TPU v7x, 32 devices: a whole 2x2x4 slice. The times are simulated.
32 devices in a mesh: dp: 4 (over y, x), expert: 4 (over z), tensor: 2 (over core).
Axes of the slice: x: 2, y: 2, z: 4, core: 2. Of those that a mesh axis runs over, the one named last changes fastest.
Arguments:
- out_grad: bfloat16 [2048, 2048], P(('dp', 'expert'), 'tensor'), may hold values from -6 to 6
- seq_ids: int32 [16, 128], P(('dp', 'expert')), may hold values from 0 to 3, never falling along the last dimension, each value on 1 to 64 neighbouring positions
- seq_weights: float32 [16, 4], P(('dp', 'expert')), may hold values from -1.5 to 1.5
- expert_ids: int32 [2048, 2], P(('dp', 'expert')), may hold values from 0 to 3, all different within a row; in each aligned block of 128 rows (0 to 127, 128 to 255, ...) at most 96 rows name the same one
- route_probs: bfloat16 [2048, 2], P(('dp', 'expert')), may hold values from 0.19921875 to 1
- down_weight: bfloat16 [4, 7168, 2048], P('expert', ('dp', 'tensor')), may hold values from -0.0625 to 0.0625
- gate_pre: bfloat16 [4, 7168, 1536], P('expert', ('dp', 'tensor')), may hold values from -6 to 6
- up_pre: bfloat16 [4, 7168, 1536], P('expert', ('dp', 'tensor')), may hold values from -6 to 6
Outputs:
- grad_gate: bfloat16 [4, 7168, 1536], P('expert', ('dp', 'tensor'))
- grad_up: bfloat16 [4, 7168, 1536], P('expert', ('dp', 'tensor'))
- grad_down: bfloat16 [4, 7168, 2048], P('expert', ('dp', 'tensor'))
- grad_probs: float32 [2048, 2], P(('dp', 'expert'))
Inputs may be any that keep to these rules, and one draw needn't show every extreme that they name: `expert_ids`: the two experts of a token differ. Among the 128 tokens of one shard no expert is named more than 96 times, and in every draw some expert is named exactly 96 times by the tokens of some shard. `seq_ids`: along a shard's row the ids never fall; each of the 4 ids names 1 to 64 tokens of the row, and one names exactly 64.
All inputs are finite; a program needn't handle non-finite values.
Results may differ from a plain program's by a relative error of at most 0.0064.
Values may be sent and summed in bfloat16 or wider, within the bound.
A program may use at most 128 MiB of HBM per device.

v0:
```python
import jax
import jax.numpy as jnp
from jax import lax
from jax.sharding import PartitionSpec as P


def silu_parts(pre_act):
    logistic = jax.nn.sigmoid(pre_act)
    return (pre_act * logistic, logistic * (1.0 + pre_act * (1.0 - logistic)))


def local(out_grad, seq_ids, seq_weights, expert_ids, route_probs, down_weight, gate_pre, up_pre):
    experts = lax.axis_size("expert")
    columns = lax.axis_size("dp")
    token_count = seq_ids.shape[1]
    capacity = gate_pre.shape[2] // (columns * experts)
    half_width = out_grad.shape[1]
    seq_count = seq_weights.shape[1]
    block_size = experts * capacity
    gate_local = gate_pre[0]
    up_local = up_pre[0]
    weight_local = down_weight[0]
    member = (seq_ids[0][:, None] == jnp.arange(seq_count, dtype=jnp.int32)[None, :]).astype(
        jnp.float32
    )
    weight_tok = jnp.sum(member * seq_weights[0][None, :], axis=1)
    scaled = (weight_tok[:, None] * out_grad.astype(jnp.float32)).astype(jnp.bfloat16)
    chosen = expert_ids.reshape(-1)
    onehot = (chosen[:, None] == jnp.arange(experts, dtype=jnp.int32)[None, :]).astype(jnp.int32)
    earlier = jnp.cumsum(onehot, axis=0) - onehot
    slot_index = chosen * capacity + jnp.sum(earlier * onehot, axis=1)
    send_rows = (
        jnp.zeros((block_size, half_width), jnp.bfloat16)
        .at[slot_index]
        .set(jnp.repeat(scaled, 2, axis=0))
    )
    send_probs = jnp.zeros((block_size,), jnp.bfloat16).at[slot_index].set(route_probs.reshape(-1))
    copies = jnp.tile(send_rows, (columns, 1))
    copy_probs = jnp.tile(send_probs, (columns,))
    arrived, arrived_probs = (
        lax.all_to_all(copies, ("dp", "expert"), split_axis=0, concat_axis=0, tiled=True),
        lax.all_to_all(copy_probs, ("dp", "expert"), split_axis=0, concat_axis=0, tiled=True),
    )
    gathered = lax.all_gather(arrived, "tensor", axis=1, tiled=True)
    gate_piece = gate_local.astype(jnp.float32)
    up_piece = up_local.astype(jnp.float32)
    activated, derivative = silu_parts(gate_piece)
    hidden = (activated * up_piece).astype(jnp.bfloat16)
    upstream = lax.dot_general(
        weight_local, gathered, (((1,), (1,)), ((), ())), preferred_element_type=jnp.float32
    )
    partial_value = jnp.sum(upstream * hidden.astype(jnp.float32), axis=0)
    grad_hidden = arrived_probs.astype(jnp.float32)[None, :] * upstream
    gate_out = (grad_hidden * up_piece * derivative).astype(jnp.bfloat16)
    up_out = (grad_hidden * activated).astype(jnp.bfloat16)
    weighted = (arrived_probs.astype(jnp.float32)[:, None] * gathered.astype(jnp.float32)).astype(
        jnp.bfloat16
    )
    grad_w = jnp.dot(hidden, weighted, preferred_element_type=jnp.float32)
    gate_acc = gate_out
    up_acc = up_out
    probe = partial_value
    grad_w, gate_acc, up_acc, probe = (grad_w, gate_acc, up_acc, probe)
    summed = lax.psum(probe, ("dp", "tensor"))
    own_totals = lax.dynamic_slice_in_dim(summed, lax.axis_index("dp") * block_size, block_size, 0)
    returned = lax.all_to_all(own_totals, "expert", split_axis=0, concat_axis=0, tiled=True)
    grad_probs = returned[slot_index].reshape(token_count, 2)
    return (gate_acc[None], up_acc[None], grad_w.astype(jnp.bfloat16)[None], grad_probs)


def solution(mesh):
    return jax.shard_map(
        local,
        mesh=mesh,
        in_specs=(
            P(("dp", "expert"), "tensor"),
            P(("dp", "expert"), None),
            P(("dp", "expert"), None),
            P(("dp", "expert"), None),
            P(("dp", "expert"), None),
            P("expert", ("dp", "tensor"), None),
            P("expert", ("dp", "tensor"), None),
            P("expert", ("dp", "tensor"), None),
        ),
        out_specs=(
            P("expert", ("dp", "tensor"), None),
            P("expert", ("dp", "tensor"), None),
            P("expert", ("dp", "tensor"), None),
            P(("dp", "expert"), None),
        ),
        check_vma=False,
    )
```

profile of v0, /device:TPU:0, one launch (start us, length us, event | category | flops | bytes accessed | tf_op | source)
XLA Modules:
  0.0 166.8 jit_solution(17966599329222551912)
XLA Ops:
  7.2 0.0 all-gather.2.cloned.1.call-start
  7.2 0.8 copy.39
  8.0 0.1 eq.44
  8.1 0.1 eq.40
  8.3 0.7 broadcast_multiply_fusion
  9.0 1.2 reduce-window.6
  10.2 0.1 slice.10
  10.3 0.1 copy.41
  10.4 0.1 copy.42
  10.5 0.1 add_bitcast_fusion
  10.6 0.1 copy.38
  10.7 0.1 mul.82
  10.8 0.8 select_reduce_fusion
  11.6 1.1 multiply_convert_fusion.5
  12.6 0.3 broadcast_in_dim.28
  12.9 0.2 reshape.128
  13.2 1.9 %scatter_custom_fusion.1 = bf16[384,1024]{1,0:T(8,128)(2,1)S(1)} fusion(s32[256]{0:T(256)S(1)} %bitcast.78, bf16[256,1024]{1,0:T(8,128)(2,1)S(1)} %reshape.128, bf16[]{:T(256)} %constant.8.clone.1), kind=kCustom, calls=%fused_computation.29 | custom fusion | bytes 786434 | tf_op jit(solution)/shard_map/scatter | solution.py:35
  15.1 0.4 tile.21
  15.5 0.0 copy-start
  15.5 0.0 copy-start.1
  15.5 80.9 %all_to_all.30 = bf16[16,96,1024]{2,1,0:T(8,128)(2,1)} all-to-all(bf16[16,96,1024]{2,1,0:T(8,128)(2,1)S(1)} %bitcast.76), channel_id=1, replica_groups=mesh['dp'=4,'expert'=4,'tensor'=2] {'dp','expert'}, dimensions={0} | all-to-all | bytes 6291456 | tf_op jit(solution)/shard_map/all_to_all | solution.py:41
  96.4 0.0 all-gather.2.cloned.1.call-update
  96.4 0.0 copy-done
  96.4 0.1 copy.43
  96.6 0.1 reshape.120
  96.7 2.2 %scatter_custom_fusion = bf16[384]{0:T(512)(128)(2,1)S(1)} fusion(s32[256]{0:T(256)S(1)} %bitcast.79, bf16[256]{0:T(256)(128)(2,1)S(1)} %reshape.120, bf16[]{:T(256)} %constant.8.clone.1), kind=kCustom, calls=%fused_computation.44 | custom fusion | bytes 770 | tf_op jit(solution)/shard_map/scatter | solution.py:37
  98.9 0.1 tile.8
  99.0 0.6 copy.44
  99.6 3.5 %all-to-all-start = ((bf16[16,96,1]{1,2,0:T(2,128)(2,1)}), bf16[16,96,1]{1,2,0:T(2,128)(2,1)S(1)}, u32[]{:S(2)}, u32[]{:S(2)}) async-start(bf16[16,96,1]{1,2,0:T(2,128)(2,1)} %copy.44), calls=%async_computation | async-start | bytes 16384 | tf_op jit(solution)/shard_map/all_to_all | solution.py:42
  103.1 7.2 %all-to-all-done = bf16[16,96,1]{1,2,0:T(2,128)(2,1)S(1)} async-done(((bf16[16,96,1]{1,2,0:T(2,128)(2,1)}), bf16[16,96,1]{1,2,0:T(2,128)(2,1)S(1)}, u32[]{:S(2)}, u32[]{:S(2)}) %all-to-all-start) | async-done | bytes 3104 | tf_op jit(solution)/shard_map/all_to_all | solution.py:42
  110.3 0.1 reshape.105
  110.4 0.2 all-gather.2.cloned.1.call-done
  110.6 0.0 copy-done.1
  110.6 14.0 %fusion.10 = (f32[1536]{0:T(1024)S(1)}, bf16[1,896,1536]{2,1,0:T(8,128)(2,1)}, bf16[1,896,1536]{2,1,0:T(8,128)(2,1)}) fusion(bf16[1,896,1536]{2,1,0:T(8,128)(2,1)S(1)} %copy-done.1, bf16[1,896,1536]{2,1,0:T(8,128)(2,1)} %param.14, f32[1536]{0:T(1024)S(1)} %reshape.105, bf16[1536,2048]{1,0:T(8,128)(2,1)} %all-gather.2.cloned.1.call-done, ...), kind=kOutput, calls=%fused_computation.21 | convolution fusion | flops 5666044416 | bytes 20983808 | tf_op jit(solution)/shard_map/dot_general | solution.py:49
  124.5 14.6 %psum.7 = f32[1536]{0:T(1024)S(1)} all-reduce(f32[1536]{0:T(1024)S(1)} %get-tuple-element.20), channel_id=1, replica_groups=mesh['dp'=4,'expert'=4,'tensor'=2] {'dp','tensor'}, use_global_device_ids=true, to_apply=%region_7.8 | all-reduce | flops 1536 | bytes 12288 | tf_op jit(solution)/shard_map/psum | solution.py:64
  139.1 0.1 dynamic_slice.3
  139.2 0.7 all_to_all.24
  139.9 4.6 %all-to-all-start.2 = ((f32[4,96,1]{1,2,0:T(1,128)}), f32[4,96,1]{1,2,0:T(1,128)S(1)}, u32[]{:S(2)}, u32[]{:S(2)}) async-start(f32[4,96,1]{1,2,0:T(1,128)} %bitcast.18), calls=%async_computation.2 | async-start | bytes 4096 | tf_op jit(solution)/shard_map/all_to_all | solution.py:66
  144.5 11.4 %convert_bitcast_fusion = bf16[1,896,2048]{2,1,0:T(8,128)(2,1)} fusion(bf16[1536,2048]{1,0:T(8,128)(2,1)} %all-gather.2.cloned.1.call-done, f32[1536]{0:T(1024)S(1)} %reshape.105, bf16[1,896,1536]{2,1,0:T(8,128)(2,1)S(1)} %copy-done.1, bf16[1,896,1536]{2,1,0:T(8,128)(2,1)} %param.14), kind=kOutput, calls=%fused_computation.25 | convolution fusion | flops 5659426816 | bytes 15472640 | tf_op jit(solution)/shard_map/dot_general | solution.py:59
  155.9 0.0 all-to-all-done.2
  155.9 0.5 broadcast.90
  156.4 0.7 reduce.7
  157.1 0.1 all_to_all.26
  157.2 1.9 %gather_fusion = f32[256]{0:T(256)S(1)} fusion(f32[384]{0:T(512)S(1)} %all_to_all.26, s32[1024]{0:T(1024)S(1)} %pad_clamp_fusion), kind=kCustom, calls=%fused_computation | custom fusion | bytes 3072 | tf_op jit(solution)/shard_map/gather | solution.py:67
  159.1 0.1 reshape.104
  159.3 0.6 copy.46
  (8 shorter events, 0.1 us)
Async XLA Ops:
  7.2 103.4 %all-gather.2.cloned.1.call-start = ((), (), s32[]{:S(2)}) async-start(), calls=%async_computation.3 | async-start | bytes 9437184 | tf_op jit(solution)/shard_map/all_gather | solution.py:44
  15.5 80.9 %copy-start = (bf16[128,2]{0,1:T(2,128)(2,1)S(1)}, bf16[128,2]{0,1:T(2,128)(2,1)}, u32[]{:S(2)}) copy-start(bf16[128,2]{0,1:T(2,128)(2,1)} %param.12) | copy-start | bytes 1540
  15.5 95.1 %copy-start.1 = (bf16[1,896,1536]{2,1,0:T(8,128)(2,1)S(1)}, bf16[1,896,1536]{2,1,0:T(8,128)(2,1)}, u32[]{:S(2)}) copy-start(bf16[1,896,1536]{2,1,0:T(8,128)(2,1)} %param.15) | copy-start | bytes 8257540
  99.6 10.7 %all-to-all-start = ((bf16[16,96,1]{1,2,0:T(2,128)(2,1)}), bf16[16,96,1]{1,2,0:T(2,128)(2,1)S(1)}, u32[]{:S(2)}, u32[]{:S(2)}) async-start(bf16[16,96,1]{1,2,0:T(2,128)(2,1)} %copy.44), calls=%async_computation | async-start | bytes 16384 | tf_op jit(solution)/shard_map/all_to_all | solution.py:42
  139.9 16.0 %all-to-all-start.2 = ((f32[4,96,1]{1,2,0:T(1,128)}), f32[4,96,1]{1,2,0:T(1,128)S(1)}, u32[]{:S(2)}, u32[]{:S(2)}) async-start(f32[4,96,1]{1,2,0:T(1,128)} %bitcast.18), calls=%async_computation.2 | async-start | bytes 4096 | tf_op jit(solution)/shard_map/all_to_all | solution.py:66
Sparse Core Ops, SparseCore 0:
  96.5 13.9 all-gather.1
where the time goes:
time: 167 us
  blocking collectives  95.4 us (57%)
  matrix products  25.4 us (15%)
  between operations  14.2 us (9%)
  local copies, waits for them, and re-layouts  11.7 us (7%)
  starting transfers between devices  8.11 us (5%)
  waiting for transfers between devices  7.37 us (4%)
  other arithmetic  4.55 us (3%)
    all_to_all x1, blocking collectives, local(): lax.all_to_all(copies, ('dp', 'expert'), split_axis=0, concat_axis=0, til...  80.9 us
    psum x1, blocking collectives, local(): summed = lax.psum(probe, ('dp', 'tensor'))  14.6 us
    dot_general x1, matrix products, local(): lax.dot_general(weight_local, gathered, (((1,), (1,)), ((), ())), preferr...  14 us
    dot_general x1, matrix products, local(): grad_w = jnp.dot(hidden, weighted, preferred_element_type=jnp.float32)  11.4 us
    all_to_all x1, waiting for transfers between devices, local(): lax.all_to_all(copy_probs, ('dp', 'expert'), split_axis=0, concat_axis=0,...  7.16 us
    all_to_all x1, starting transfers between devices, local(): lax.all_to_all(own_totals, 'expert', split_axis=0, concat_axis=0, tiled=T...  4.59 us
    all_to_all x1, starting transfers between devices, local(): lax.all_to_all(copy_probs, ('dp', 'expert'), split_axis=0, concat_axis=0,...  3.48 us
  transfers between devices with their start and end apart: 3, of which 2 were waited for; matrix products, arithmetic and copies ran while one was open for 9% of the time, Pallas kernels for 0%

commit v1 on v0

--- a/solution.py
+++ b/solution.py
@@ -61,7 +61,8 @@
     up_acc = up_out
     probe = partial_value
     grad_w, gate_acc, up_acc, probe = (grad_w, gate_acc, up_acc, probe)
-    summed = lax.psum(probe, ("dp", "tensor"))
+    parts = lax.all_gather(probe, ("dp", "tensor"), axis=0, tiled=False)
+    summed = parts.sum(axis=0)
     own_totals = lax.dynamic_slice_in_dim(summed, lax.axis_index("dp") * block_size, block_size, 0)
     returned = lax.all_to_all(own_totals, "expert", split_axis=0, concat_axis=0, tiled=True)
     grad_probs = returned[slot_index].reshape(token_count, 2)

time: 167 us -> 162 us (0.970)
  blocking collectives: 95.4 us -> 90.3 us
    psum x1 -> x0, blocking collectives: 14.6 us -> none  [local(): summed = lax.psum(probe, ('dp', 'tensor'))]
    all_gather x0 -> x1, blocking collectives: none -> 9.41 us  [local(): parts = lax.all_gather(probe, ('dp', 'tensor'), axis=0, tiled=False)]
where the time goes in v1:
time: 162 us
  blocking collectives  90.3 us (56%)
  matrix products  25.4 us (16%)
  between operations  14.2 us (9%)
  local copies, waits for them, and re-layouts  11.7 us (7%)
  starting transfers between devices  8.12 us (5%)
  waiting for transfers between devices  7.37 us (5%)
  other arithmetic  4.59 us (3%)
    all_to_all x1, blocking collectives, local(): lax.all_to_all(copies, ('dp', 'expert'), split_axis=0, concat_axis=0, til...  80.9 us
    dot_general x1, matrix products, local(): lax.dot_general(weight_local, gathered, (((1,), (1,)), ((), ())), preferr...  14 us
    dot_general x1, matrix products, local(): grad_w = jnp.dot(hidden, weighted, preferred_element_type=jnp.float32)  11.4 us
    all_gather x1, blocking collectives, local(): parts = lax.all_gather(probe, ('dp', 'tensor'), axis=0, tiled=False)  9.41 us
    all_to_all x1, waiting for transfers between devices, local(): lax.all_to_all(copy_probs, ('dp', 'expert'), split_axis=0, concat_axis=0,...  7.16 us
    all_to_all x1, starting transfers between devices, local(): lax.all_to_all(own_totals, 'expert', split_axis=0, concat_axis=0, tiled=T...  4.61 us
    all_to_all x1, starting transfers between devices, local(): lax.all_to_all(copy_probs, ('dp', 'expert'), split_axis=0, concat_axis=0,...  3.48 us
  transfers between devices with their start and end apart: 3, of which 2 were waited for; matrix products, arithmetic and copies ran while one was open for 9% of the time, Pallas kernels for 0%

profile of v1, /device:TPU:0, one launch (start us, length us, event | category | flops | bytes accessed | tf_op | source)
XLA Modules:
  0.0 161.7 jit_solution(16693667524796966703)
XLA Ops:
  7.2 0.0 all-gather.4.cloned.1.call-start
  7.2 0.8 copy.39
  8.0 0.1 eq.44
  8.1 0.1 eq.40
  8.3 0.7 broadcast_multiply_fusion
  9.0 1.2 reduce-window.6
  10.2 0.1 slice.10
  10.3 0.1 copy.41
  10.4 0.1 copy.42
  10.5 0.1 add_bitcast_fusion
  10.6 0.1 copy.38
  10.7 0.1 mul.82
  10.8 0.8 select_reduce_fusion
  11.6 1.1 multiply_convert_fusion.5
  12.6 0.3 broadcast_in_dim.28
  12.9 0.2 reshape.128
  13.2 1.9 %scatter_custom_fusion.1 = bf16[384,1024]{1,0:T(8,128)(2,1)S(1)} fusion(s32[256]{0:T(256)S(1)} %bitcast.78, bf16[256,1024]{1,0:T(8,128)(2,1)S(1)} %reshape.128, bf16[]{:T(256)} %constant.8.clone.1), kind=kCustom, calls=%fused_computation.29 | custom fusion | bytes 786434 | tf_op jit(solution)/shard_map/scatter | solution.py:35
  15.1 0.4 tile.21
  15.5 0.0 copy-start
  15.5 0.0 copy-start.1
  15.5 80.9 %all_to_all.30 = bf16[16,96,1024]{2,1,0:T(8,128)(2,1)} all-to-all(bf16[16,96,1024]{2,1,0:T(8,128)(2,1)S(1)} %bitcast.76), channel_id=1, replica_groups=mesh['dp'=4,'expert'=4,'tensor'=2] {'dp','expert'}, dimensions={0} | all-to-all | bytes 6291456 | tf_op jit(solution)/shard_map/all_to_all | solution.py:41
  96.4 0.0 all-gather.4.cloned.1.call-update
  96.4 0.0 copy-done
  96.4 0.1 copy.43
  96.6 0.1 reshape.120
  96.7 2.2 %scatter_custom_fusion = bf16[384]{0:T(512)(128)(2,1)S(1)} fusion(s32[256]{0:T(256)S(1)} %bitcast.79, bf16[256]{0:T(256)(128)(2,1)S(1)} %reshape.120, bf16[]{:T(256)} %constant.8.clone.1), kind=kCustom, calls=%fused_computation.44 | custom fusion | bytes 770 | tf_op jit(solution)/shard_map/scatter | solution.py:37
  98.9 0.1 tile.8
  99.0 0.6 copy.44
  99.6 3.5 %all-to-all-start = ((bf16[16,96,1]{1,2,0:T(2,128)(2,1)}), bf16[16,96,1]{1,2,0:T(2,128)(2,1)S(1)}, u32[]{:S(2)}, u32[]{:S(2)}) async-start(bf16[16,96,1]{1,2,0:T(2,128)(2,1)} %copy.44), calls=%async_computation | async-start | bytes 16384 | tf_op jit(solution)/shard_map/all_to_all | solution.py:42
  103.1 7.2 %all-to-all-done = bf16[16,96,1]{1,2,0:T(2,128)(2,1)S(1)} async-done(((bf16[16,96,1]{1,2,0:T(2,128)(2,1)}), bf16[16,96,1]{1,2,0:T(2,128)(2,1)S(1)}, u32[]{:S(2)}, u32[]{:S(2)}) %all-to-all-start) | async-done | bytes 3104 | tf_op jit(solution)/shard_map/all_to_all | solution.py:42
  110.3 0.1 reshape.105
  110.4 0.2 all-gather.4.cloned.1.call-done
  110.6 0.0 copy-done.1
  110.6 14.0 %fusion.10 = (f32[1536]{0:T(1024)S(1)}, bf16[1,896,1536]{2,1,0:T(8,128)(2,1)}, bf16[1,896,1536]{2,1,0:T(8,128)(2,1)}) fusion(bf16[1,896,1536]{2,1,0:T(8,128)(2,1)S(1)} %copy-done.1, bf16[1,896,1536]{2,1,0:T(8,128)(2,1)} %param.14, f32[1536]{0:T(1024)S(1)} %reshape.105, bf16[1536,2048]{1,0:T(8,128)(2,1)} %all-gather.4.cloned.1.call-done, ...), kind=kOutput, calls=%fused_computation.21 | convolution fusion | flops 5666044416 | bytes 20983808 | tf_op jit(solution)/shard_map/dot_general | solution.py:49
  124.5 9.4 %all-gather.1 = f32[8,1,1536]{2,1,0:T(1,128)S(1)} all-gather(f32[1,1,1536]{2,1,0:T(1,128)S(1)} %reshape.133), channel_id=2, replica_groups=mesh['dp'=4,'expert'=4,'tensor'=2] {'dp','tensor'}, dimensions={0}, use_global_device_ids=true | all-gather | bytes 55296 | tf_op jit(solution)/shard_map/all_gather | solution.py:64
  134.0 0.1 dynamic_slice.3
  134.1 0.7 all_to_all.24
  134.8 4.6 %all-to-all-start.2 = ((f32[4,96,1]{1,2,0:T(1,128)}), f32[4,96,1]{1,2,0:T(1,128)S(1)}, u32[]{:S(2)}, u32[]{:S(2)}) async-start(f32[4,96,1]{1,2,0:T(1,128)} %bitcast.18), calls=%async_computation.2 | async-start | bytes 4096 | tf_op jit(solution)/shard_map/all_to_all | solution.py:67
  139.4 11.4 %convert_bitcast_fusion = bf16[1,896,2048]{2,1,0:T(8,128)(2,1)} fusion(bf16[1536,2048]{1,0:T(8,128)(2,1)} %all-gather.4.cloned.1.call-done, f32[1536]{0:T(1024)S(1)} %reshape.105, bf16[1,896,1536]{2,1,0:T(8,128)(2,1)S(1)} %copy-done.1, bf16[1,896,1536]{2,1,0:T(8,128)(2,1)} %param.14), kind=kOutput, calls=%fused_computation.25 | convolution fusion | flops 5659426816 | bytes 15472640 | tf_op jit(solution)/shard_map/dot_general | solution.py:59
  150.8 0.0 all-to-all-done.2
  150.8 0.5 broadcast.90
  151.3 0.7 reduce.8
  152.0 0.1 all_to_all.26
  152.1 1.9 %gather_fusion = f32[256]{0:T(256)S(1)} fusion(f32[384]{0:T(512)S(1)} %all_to_all.26, s32[1024]{0:T(1024)S(1)} %pad_clamp_fusion), kind=kCustom, calls=%fused_computation | custom fusion | bytes 3072 | tf_op jit(solution)/shard_map/gather | solution.py:68
  154.0 0.1 reshape.104
  154.2 0.6 copy.46
  (10 shorter events, 0.2 us)
Async XLA Ops:
  7.2 103.4 %all-gather.4.cloned.1.call-start = ((), (), s32[]{:S(2)}) async-start(), calls=%async_computation.3 | async-start | bytes 9437184 | tf_op jit(solution)/shard_map/all_gather | solution.py:44
  15.5 80.9 %copy-start = (bf16[128,2]{0,1:T(2,128)(2,1)S(1)}, bf16[128,2]{0,1:T(2,128)(2,1)}, u32[]{:S(2)}) copy-start(bf16[128,2]{0,1:T(2,128)(2,1)} %param.12) | copy-start | bytes 1540
  15.5 95.1 %copy-start.1 = (bf16[1,896,1536]{2,1,0:T(8,128)(2,1)S(1)}, bf16[1,896,1536]{2,1,0:T(8,128)(2,1)}, u32[]{:S(2)}) copy-start(bf16[1,896,1536]{2,1,0:T(8,128)(2,1)} %param.15) | copy-start | bytes 8257540
  99.6 10.7 %all-to-all-start = ((bf16[16,96,1]{1,2,0:T(2,128)(2,1)}), bf16[16,96,1]{1,2,0:T(2,128)(2,1)S(1)}, u32[]{:S(2)}, u32[]{:S(2)}) async-start(bf16[16,96,1]{1,2,0:T(2,128)(2,1)} %copy.44), calls=%async_computation | async-start | bytes 16384 | tf_op jit(solution)/shard_map/all_to_all | solution.py:42
  134.8 16.0 %all-to-all-start.2 = ((f32[4,96,1]{1,2,0:T(1,128)}), f32[4,96,1]{1,2,0:T(1,128)S(1)}, u32[]{:S(2)}, u32[]{:S(2)}) async-start(f32[4,96,1]{1,2,0:T(1,128)} %bitcast.18), calls=%async_computation.2 | async-start | bytes 4096 | tf_op jit(solution)/shard_map/all_to_all | solution.py:67
Sparse Core Ops, SparseCore 0:
  96.5 13.9 all-gather.3
